TPU v7x, 32 devices: a whole 2x2x4 slice. The times are simulated.
32 devices in a mesh: dp: 8 (over y, x, core), tensor: 4 (over z).
Axes of the slice: x: 2, y: 2, z: 4, core: 2. Of those that a mesh axis runs over, the one named last changes fastest.
Arguments:
- saved_input: bfloat16 [2048, 6144], P('dp', 'tensor'), may hold values from -6 to 6
- queries: bfloat16 [2048, 1024], P('dp', 'tensor'), may hold values from -8 to 8
- keys: bfloat16 [2048, 1024], P('dp', 'tensor'), may hold values from -8 to 8
- value_weight: bfloat16 [6144, 1024], P(None, 'tensor'), may hold values from -0.109375 to 0.109375
- grad_attended: bfloat16 [2048, 1024], P('dp', 'tensor'), may hold values from -6 to 6
Outputs:
- grad_input: bfloat16 [2048, 6144], P('dp', 'tensor')
- grad_value_weight: float32 [6144, 1024], P('dp', 'tensor')
- grad_queries: bfloat16 [2048, 1024], P('dp', 'tensor')
- grad_keys: bfloat16 [2048, 1024], P('dp', 'tensor')
All inputs are finite; a program needn't handle non-finite values.
Results may differ from a plain program's by a relative error of at most 0.02.
Values may be sent and summed in bfloat16 or wider, within the bound.
A program may use at most 64 MiB of HBM per device.

v0:
```python
import jax
import jax.numpy as jnp
from jax import lax
from jax.sharding import PartitionSpec as P

HD = 128


def on_device(saved_input, queries, keys, value_weight, grad_attended):
    token_count = queries.shape[0]
    local_width = value_weight.shape[1]
    local_heads = local_width // HD
    score_scale = 1.0 / jnp.sqrt(jnp.float32(HD))
    full_input = lax.all_gather(saved_input, "tensor", axis=1, tiled=True)
    values = jnp.dot(full_input, value_weight, preferred_element_type=jnp.float32).astype(
        jnp.bfloat16
    )
    query_heads = queries.reshape(token_count, local_heads, HD)
    key_heads = keys.reshape(token_count, local_heads, HD)
    value_heads = values.reshape(token_count, local_heads, HD)
    grad_heads = grad_attended.reshape(token_count, local_heads, HD)
    scores = (
        jnp.einsum("qhd,khd->hqk", query_heads, key_heads, preferred_element_type=jnp.float32)
        * score_scale
    )
    positions = lax.iota(jnp.int32, token_count)
    causal = positions[:, None] >= positions[None, :]
    scores = jnp.where(causal[None], scores, -jnp.inf)
    row_max = jnp.max(scores, axis=-1, keepdims=True)
    weights_exp = jnp.exp(scores - row_max)
    attention = weights_exp / jnp.sum(weights_exp, axis=-1, keepdims=True)
    probs_half = attention.astype(jnp.bfloat16)
    grad_values = jnp.einsum(
        "hqk,qhd->khd", probs_half, grad_heads, preferred_element_type=jnp.float32
    ).astype(jnp.bfloat16)
    grad_probs = jnp.einsum(
        "qhd,khd->hqk", grad_heads, value_heads, preferred_element_type=jnp.float32
    )
    row_dot = jnp.sum(attention * grad_probs, axis=-1, keepdims=True)
    grad_scores = (attention * (grad_probs - row_dot) * score_scale).astype(jnp.bfloat16)
    grad_queries = jnp.einsum(
        "hqk,khd->qhd", grad_scores, key_heads, preferred_element_type=jnp.float32
    ).astype(jnp.bfloat16)
    grad_keys = jnp.einsum(
        "hqk,qhd->khd", grad_scores, query_heads, preferred_element_type=jnp.float32
    ).astype(jnp.bfloat16)
    value_flat = grad_values.reshape(token_count, local_width)
    data_groups = lax.axis_size("dp")
    partial_value = lax.dot_general(
        value_flat, value_weight, (((1,), (1,)), ((), ())), preferred_element_type=jnp.float32
    )
    grad_input = lax.psum_scatter(
        partial_value.astype(jnp.bfloat16), "tensor", scatter_dimension=1, tiled=True
    )
    partial_value = lax.dot_general(
        full_input, value_flat, (((0,), (0,)), ((), ())), preferred_element_type=jnp.float32
    )
    summed = lax.psum_scatter(
        partial_value.astype(jnp.bfloat16), "dp", scatter_dimension=0, tiled=True
    ).astype(jnp.float32)
    grad_value_weight = summed / jnp.float32(data_groups)
    return (
        grad_input,
        grad_value_weight,
        grad_queries.reshape(token_count, local_width),
        grad_keys.reshape(token_count, local_width),
    )


def solution(mesh):
    placed = (
        P("dp", "tensor"),
        P("dp", "tensor"),
        P("dp", "tensor"),
        P(None, "tensor"),
        P("dp", "tensor"),
    )
    return jax.shard_map(
        on_device,
        mesh=mesh,
        in_specs=placed,
        out_specs=(P("dp", "tensor"), P("dp", "tensor"), P("dp", "tensor"), P("dp", "tensor")),
        check_vma=False,
    )
```

profile of v0, /device:TPU:0, one launch (start us, length us, event | category | flops | bytes accessed | tf_op | source)
XLA Modules:
  0.0 195.0 jit_solution(18344579385633237910)
XLA Ops:
  7.2 0.0 copy-start
  7.2 0.0 all-gather.2.cloned.1.call-start
  7.2 0.7 all-gather.2.cloned.1.call-update
  7.9 0.0 reduce-scatter.5.cloned.1.call-start
  8.0 1.2 copy.26
  9.1 1.0 copy.27
  10.2 0.0 copy-start.2
  10.2 1.2 fusion.28
  11.3 0.0 copy-done.2
  11.3 1.5 convolution_convert_fusion.4
  12.9 62.9 %all-gather.2.cloned.1.call-done = bf16[256,6144]{1,0:T(8,128)(2,1)} async-done(((bf16[256,1536]{1,0:T(8,128)(2,1)}), bf16[256,6144]{1,0:T(8,128)(2,1)}) %all-gather.2.cloned.1.call-update) | async-done | bytes 3145744 | tf_op jit(solution)/shard_map/all_gather | solution.py:14
  75.8 4.6 %fusion.2 = bf16[6144,256]{0,1:T(8,128)(2,1)} fusion(bf16[256,256]{0,1:T(8,128)(2,1)S(1)} %bitcast.41, bf16[256,6144]{1,0:T(8,128)(2,1)} %all-gather.2.cloned.1.call-done), kind=kOutput, calls=%fused_computation.4 | convolution fusion | flops 806879232 | bytes 6422528 | tf_op jit(solution)/shard_map/dot_general | solution.py:55
  80.3 0.0 reduce-scatter.5.cloned.1.call-update
  80.4 0.0 reduce-scatter.3.cloned.1.call-start
  80.4 0.0 copy-done
  80.4 2.7 %convolution_convert_fusion.1 = bf16[256,6144]{1,0:T(8,128)(2,1)} fusion(bf16[256,256]{0,1:T(8,128)(2,1)S(1)} %bitcast.42, bf16[6144,256]{1,0:T(8,128)(2,1)S(1)} %copy-done), kind=kOutput, calls=%fused_computation.3 | convolution fusion | flops 806879232 | bytes 6422528 | tf_op jit(solution)/shard_map/dot_general | solution.py:49
  83.1 0.0 reduce-scatter.3.cloned.1.call-update
  83.2 0.0 copy-start.1
  83.2 3.5 %convolution_convert_fusion.5 = bf16[256,256]{0,1:T(8,128)(2,1)S(1)} fusion(bf16[256,6144]{1,0:T(8,128)(2,1)} %all-gather.2.cloned.1.call-done, bf16[6144,256]{1,0:T(8,128)(2,1)S(1)} %copy-done), kind=kOutput, calls=%fused_computation.17 | convolution fusion | flops 805371904 | bytes 6422528 | tf_op jit(solution)/shard_map/dot_general | solution.py:15
  86.7 0.0 copy-done.1
  86.7 1.1 convolution_bitcast_fusion
  87.8 2.0 %convolution_convert_fusion.2 = bf16[2,256,128]{1,2,0:T(8,128)(2,1)S(1)} fusion(bf16[256,2,128]{0,2,1:T(8,128)(2,1)S(1)} %bitcast.49, f32[2,256,256]{1,2,0:T(8,128)} %convolution_bitcast_fusion, f32[2,256,256]{1,2,0:T(8,128)} %get-tuple-element.9, f32[2,256]{1,0:T(2,128)S(1)} %get-tuple-element.8), kind=kOutput, calls=%fused_computation.14 | convolution fusion | flops 34538240 | bytes 1312768 | tf_op jit(solution)/shard_map/hqk,khd->qhd/dot_general | solution.py:41
  89.7 0.8 copy.20
  90.5 2.0 %convolution_convert_fusion.3 = bf16[2,256,128]{1,2,0:T(8,128)(2,1)S(1)} fusion(bf16[256,2,128]{0,2,1:T(8,128)(2,1)S(1)} %bitcast.46, f32[2,256,256]{1,2,0:T(8,128)} %convolution_bitcast_fusion, f32[2,256,256]{1,2,0:T(8,128)} %get-tuple-element.9, f32[2,256]{1,0:T(2,128)S(1)} %get-tuple-element.8), kind=kOutput, calls=%fused_computation.15 | convolution fusion | flops 34538240 | bytes 1312768 | tf_op jit(solution)/shard_map/hqk,qhd->khd/dot_general | solution.py:44
  92.5 0.8 copy.21
  93.2 32.0 %reduce-scatter.5.cloned.1.call-done = bf16[768,256]{0,1:T(8,128)(2,1)} async-done(((bf16[6144,256]{0,1:T(8,128)(2,1)}), bf16[768,256]{0,1:T(8,128)(2,1)}) %reduce-scatter.5.cloned.1.call-update) | async-done | bytes 393232 | tf_op jit(solution)/shard_map/reduce_scatter | solution.py:58
  125.2 1.9 convert_multiply_fusion
  127.1 2.3 %copy.19 = f32[768,256]{1,0:T(8,128)} copy(f32[768,256]{0,1:T(8,128)} %convert_multiply_fusion) | data formatting | bytes 1572864
  129.4 59.1 %reduce-scatter.3.cloned.1.call-done = bf16[256,1536]{1,0:T(8,128)(2,1)} async-done(((bf16[256,6144]{1,0:T(8,128)(2,1)}), bf16[256,1536]{1,0:T(8,128)(2,1)}) %reduce-scatter.3.cloned.1.call-update) | async-done | bytes 786448 | tf_op jit(solution)/shard_map/reduce_scatter | solution.py:52
  (1 shorter events, 0.0 us)
Async XLA Ops:
  7.2 73.2 %copy-start = (bf16[6144,256]{1,0:T(8,128)(2,1)S(1)}, bf16[6144,256]{1,0:T(8,128)(2,1)}, u32[]{:S(2)}) copy-start(bf16[6144,256]{1,0:T(8,128)(2,1)} %param.8) | copy-start | bytes 9437188
  7.2 68.6 %all-gather.2.cloned.1.call-start = ((), (), s32[]{:S(2)}) async-start(), calls=%async_computation.3 | async-start | bytes 3932160 | tf_op jit(solution)/shard_map/all_gather | solution.py:14
  7.9 117.3 %reduce-scatter.5.cloned.1.call-start = ((), (), s32[]{:S(2)}) async-start(), calls=%async_computation.4 | async-start | bytes 3538944 | tf_op jit(solution)/shard_map/reduce_scatter | solution.py:58
  10.2 1.2 copy-start.2
  80.4 108.1 %reduce-scatter.3.cloned.1.call-start = ((), (), s32[]{:S(2)}) async-start(), calls=%async_computation.2 | async-start | bytes 3932160 | tf_op jit(solution)/shard_map/reduce_scatter | solution.py:52
  83.2 3.5 %copy-start.1 = (bf16[256,256]{1,0:T(8,128)(2,1)S(1)}, bf16[256,256]{1,0:T(8,128)(2,1)}, u32[]{:S(2)}) copy-start(bf16[256,256]{1,0:T(8,128)(2,1)} %param.9) | copy-start | bytes 393220
Sparse Core Ops, SparseCore 0:
  9.6 66.1 all-gather.1
  80.5 44.6 reduce-scatter.4
  128.1 60.3 reduce-scatter.2
where the time goes:
time: 195 us
  waiting for transfers between devices  155 us (79%)
  matrix products  18.5 us (9%)
  between operations  13.8 us (7%)
  local copies, waits for them, and re-layouts  5.98 us (3%)
  other arithmetic  1.95 us (1%)
    all_gather x1, waiting for transfers between devices, on_device(): full_input = lax.all_gather(saved_input, 'tensor', axis=1, tiled=True)  62.9 us
    reduce_scatter x1, waiting for transfers between devices, on_device(): lax.psum_scatter(partial_value.astype(jnp.bfloat16), 'tensor', scatter_di...  59.1 us
    reduce_scatter x1, waiting for transfers between devices, on_device(): lax.psum_scatter(partial_value.astype(jnp.bfloat16), 'dp', scatter_dimens...  32 us
    dot_general x1, matrix products, on_device(): lax.dot_general(full_input, value_flat, (((0,), (0,)), ((), ())), preferr...  4.58 us
  transfers between devices with their start and end apart: 3, of which 3 were waited for; matrix products, arithmetic and copies ran while one was open for 11% of the time, Pallas kernels for 0%

commit v1 on v0

--- a/solution.py
+++ b/solution.py
@@ -11,7 +11,7 @@
     local_width = value_weight.shape[1]
     local_heads = local_width // HD
     score_scale = 1.0 / jnp.sqrt(jnp.float32(HD))
-    full_input = lax.all_gather(saved_input, "tensor", axis=1, tiled=True)
+    full_input = jnp.concatenate(lax.all_gather(saved_input, "tensor"), axis=1)
     values = jnp.dot(full_input, value_weight, preferred_element_type=jnp.float32).astype(
         jnp.bfloat16
     )

time: 195 us -> 200 us (1.026)
  local copies, waits for them, and re-layouts: 5.98 us -> 10.7 us
    reshape x0 -> x1, local copies, waits for them, and re-layouts: none -> 4.73 us  [on_device(): full_input = jnp.concatenate(lax.all_gather(saved_input, 'tensor'), axis=1)]
where the time goes in v1:
time: 200 us
  waiting for transfers between devices  155 us (78%)
  matrix products  18.5 us (9%)
  between operations  13.8 us (7%)
  local copies, waits for them, and re-layouts  10.7 us (5%)
    all_gather x1, waiting for transfers between devices, on_device(): full_input = jnp.concatenate(lax.all_gather(saved_input, 'tensor'), axis=1)  62.9 us
    reduce_scatter x1, waiting for transfers between devices, on_device(): lax.psum_scatter(partial_value.astype(jnp.bfloat16), 'tensor', scatter_di...  59.1 us
    reduce_scatter x1, waiting for transfers between devices, on_device(): lax.psum_scatter(partial_value.astype(jnp.bfloat16), 'dp', scatter_dimens...  32 us
    reshape x1, local copies, waits for them, and re-layouts, on_device(): full_input = jnp.concatenate(lax.all_gather(saved_input, 'tensor'), axis=1)  4.73 us
    dot_general x1, matrix products, on_device(): lax.dot_general(full_input, value_flat, (((0,), (0,)), ((), ())), preferr...  4.61 us
  transfers between devices with their start and end apart: 3, of which 3 were waited for; matrix products, arithmetic and copies ran while one was open for 11% of the time, Pallas kernels for 0%

profile of v1, /device:TPU:0, one launch (start us, length us, event | category | flops | bytes accessed | tf_op | source)
XLA Modules:
  0.0 199.8 jit_solution(5724853048283546005)
XLA Ops:
  7.2 0.0 copy-start
  7.2 0.0 all-gather.3.cloned.1.call-start
  7.2 0.7 all-gather.3.cloned.1.call-update
  7.9 0.0 reduce-scatter.5.cloned.1.call-start
  8.0 1.2 copy.53
  9.1 1.0 copy.54
  10.2 0.0 copy-start.2
  10.2 1.2 fusion.28
  11.3 0.0 copy-done.2
  11.3 1.5 convolution_convert_fusion.4
  12.9 62.9 %all-gather.3.cloned.1.call-done = bf16[1024,1536]{1,0:T(8,128)(2,1)} async-done(((bf16[256,1536]{1,0:T(8,128)(2,1)}), bf16[1024,1536]{1,0:T(8,128)(2,1)}) %all-gather.3.cloned.1.call-update) | async-done | bytes 3145744 | tf_op jit(solution)/shard_map/all_gather | solution.py:14
  75.8 4.7 %copy.39 = bf16[256,4,1536]{0,2,1:T(8,128)(2,1)} copy(bf16[256,4,1536]{2,0,1:T(8,128)(2,1)} %bitcast.47) | data formatting | bytes 6291456 | tf_op jit(solution)/shard_map/reshape | solution.py:14
  80.5 4.6 %fusion.2 = bf16[6144,256]{0,1:T(8,128)(2,1)} fusion(bf16[256,256]{0,1:T(8,128)(2,1)S(1)} %bitcast.48, bf16[256,6144]{0,1:T(8,128)(2,1)} %bitcast.45), kind=kOutput, calls=%fused_computation.4 | convolution fusion | flops 806879232 | bytes 6422528 | tf_op jit(solution)/shard_map/dot_general | solution.py:55
  85.1 0.0 reduce-scatter.5.cloned.1.call-update
  85.1 0.0 reduce-scatter.3.cloned.1.call-start
  85.2 0.0 copy-done
  85.2 2.7 %convolution_convert_fusion.1 = bf16[256,6144]{1,0:T(8,128)(2,1)} fusion(bf16[256,256]{0,1:T(8,128)(2,1)S(1)} %bitcast.49, bf16[6144,256]{1,0:T(8,128)(2,1)S(1)} %copy-done), kind=kOutput, calls=%fused_computation.3 | convolution fusion | flops 806879232 | bytes 6422528 | tf_op jit(solution)/shard_map/dot_general | solution.py:49
  87.9 0.0 reduce-scatter.3.cloned.1.call-update
  87.9 0.0 copy-start.1
  87.9 3.5 %convolution_convert_fusion.5 = bf16[256,256]{0,1:T(8,128)(2,1)S(1)} fusion(bf16[256,6144]{0,1:T(8,128)(2,1)} %bitcast.46, bf16[6144,256]{1,0:T(8,128)(2,1)S(1)} %copy-done), kind=kOutput, calls=%fused_computation.17 | convolution fusion | flops 805371904 | bytes 6422528 | tf_op jit(solution)/shard_map/dot_general | solution.py:15
  91.4 0.0 copy-done.1
  91.5 1.1 convolution_bitcast_fusion
  92.5 2.0 convolution_convert_fusion.2
  94.5 0.8 copy.47
  95.3 2.0 convolution_convert_fusion.3
  97.2 0.8 copy.48
  98.0 32.0 %reduce-scatter.5.cloned.1.call-done = bf16[768,256]{0,1:T(8,128)(2,1)} async-done(((bf16[6144,256]{0,1:T(8,128)(2,1)}), bf16[768,256]{0,1:T(8,128)(2,1)}) %reduce-scatter.5.cloned.1.call-update) | async-done | bytes 393232 | tf_op jit(solution)/shard_map/reduce_scatter | solution.py:58
  129.9 1.9 convert_multiply_fusion
  131.9 2.3 %copy.46 = f32[768,256]{1,0:T(8,128)} copy(f32[768,256]{0,1:T(8,128)} %convert_multiply_fusion) | data formatting | bytes 1572864
  134.2 59.1 %reduce-scatter.3.cloned.1.call-done = bf16[256,1536]{1,0:T(8,128)(2,1)} async-done(((bf16[256,6144]{1,0:T(8,128)(2,1)}), bf16[256,1536]{1,0:T(8,128)(2,1)}) %reduce-scatter.3.cloned.1.call-update) | async-done | bytes 786448 | tf_op jit(solution)/shard_map/reduce_scatter | solution.py:52
  (1 shorter events, 0.0 us)
Async XLA Ops:
  7.2 78.0 %copy-start = (bf16[6144,256]{1,0:T(8,128)(2,1)S(1)}, bf16[6144,256]{1,0:T(8,128)(2,1)}, u32[]{:S(2)}) copy-start(bf16[6144,256]{1,0:T(8,128)(2,1)} %param.8) | copy-start | bytes 9437188
  7.2 68.6 %all-gather.3.cloned.1.call-start = ((), (), s32[]{:S(2)}) async-start(), calls=%async_computation.4 | async-start | bytes 3932160 | tf_op jit(solution)/shard_map/all_gather | solution.py:14
  7.9 122.0 %reduce-scatter.5.cloned.1.call-start = ((), (), s32[]{:S(2)}) async-start(), calls=%async_computation.3 | async-start | bytes 3538944 | tf_op jit(solution)/shard_map/reduce_scatter | solution.py:58
  10.2 1.2 copy-start.2
  85.1 108.1 %reduce-scatter.3.cloned.1.call-start = ((), (), s32[]{:S(2)}) async-start(), calls=%async_computation.2 | async-start | bytes 3932160 | tf_op jit(solution)/shard_map/reduce_scatter | solution.py:52
  87.9 3.5 %copy-start.1 = (bf16[256,256]{1,0:T(8,128)(2,1)S(1)}, bf16[256,256]{1,0:T(8,128)(2,1)}, u32[]{:S(2)}) copy-start(bf16[256,256]{1,0:T(8,128)(2,1)} %param.9) | copy-start | bytes 393220
Sparse Core Ops, SparseCore 0:
  9.6 66.1 all-gather.2
  85.2 44.6 reduce-scatter.4
  132.8 60.3 reduce-scatter.2
